TPU v7x, 128 devices: a whole 4x4x4 slice. The times are simulated.
128 devices in a mesh: gx: 8 (over y, core), gy: 16 (over z, x).
Axes of the slice: x: 4, y: 4, z: 4, core: 2. Of those that a mesh axis runs over, the one named last changes fastest.
Arguments:
- a_rows: bfloat16 [786432, 1024], P(('gx', 'gy')), may hold values from -24 to 24
- heights: int32 [128], P('gx'), may hold values from 1 to 44, as said below
- destination: int32 [128, 48], P('gx'), may hold values from 0 to 4095, as said below
Outputs:
- ortho_rows: bfloat16 [524288, 1024], P(('gx', 'gy'))
- factor_r: float32 [1024, 1024], replicated
Inputs may be any that keep to these rules, and one draw needn't show every extreme that they name: Tiles 0 to heights[d] - 1 of device d are live, the others carry nothing of the problem; the largest value is reached in every draw. For a live tile, destination // 32 is a device with the same gx index as the tile's device; live tiles name distinct slots; one device sends at most one live tile to any other device; entries of tiles that are not live are meaningless.
All inputs are finite; a program needn't handle non-finite values.
Results may differ from a plain program's by a relative error of at most 0.00055.
Values may be sent and summed in bfloat16 or wider, within the bound.
No kernel may reach another device: no remote copies, remote signals or barrier semaphores. Data moves between devices by JAX's collectives and lax.ppermute only.
A program may use at most 256 MiB of HBM per device.

v0:
```python
import math

import jax
import jax.numpy as jnp
from jax import lax
from jax.sharding import PartitionSpec as P

TILE = 128
SLOTS = 32


def factor(row_block):
    gram_local = lax.dot_general(
        row_block, row_block, (((0,), (0,)), ((), ())), preferred_element_type=jnp.float32
    )
    summed = lax.psum(gram_local, ("gx", "gy"))
    return jnp.linalg.cholesky(summed)


def normalise(low_factor, row_block, root_scale):
    solved = jax.scipy.linalg.solve_triangular(
        low_factor, row_block.astype(jnp.float32).T, lower=True
    )
    return (solved.T * root_scale).astype(jnp.bfloat16)


def on_device(a_rows, heights, destination):
    breadth = a_rows.shape[1]
    size_gy = lax.axis_size("gy")
    devices = lax.axis_size("gx") * size_gy
    group_pos = lax.axis_index("gy")
    my_index = lax.axis_index("gx") * size_gy + group_pos
    group_base = my_index - group_pos
    tile_stack = a_rows.reshape(-1, TILE, breadth)
    stored = tile_stack.shape[0]
    tile_ids = jnp.arange(stored, dtype=jnp.int32)
    peer_ids = jnp.arange(size_gy, dtype=jnp.int32)
    slot_ids = jnp.arange(SLOTS, dtype=jnp.int32)
    tile_live = tile_ids[None, :] < heights[:, None]
    target_dev = destination // SLOTS
    target_slot = destination % SLOTS
    own_live = tile_live[group_pos]
    own_dev = target_dev[group_pos]
    own_slot = target_slot[group_pos]
    leaving = own_live & (own_dev != my_index)
    chosen = leaving[None, :] & (own_dev[None, :] - group_base == peer_ids[:, None])
    send_index = jnp.sum(jnp.where(chosen, tile_ids[None, :], 0), axis=1)
    send_has = jnp.any(chosen, axis=1)
    arriving = tile_live & (target_dev == my_index) & (peer_ids[:, None] != group_pos)
    arrive_slot = jnp.sum(jnp.where(arriving, target_slot, 0), axis=1)
    arrive_has = jnp.any(arriving, axis=1)
    staying = own_live & (own_dev == my_index)
    own_match = staying[None, :] & (own_slot[None, :] == slot_ids[:, None])
    in_match = arrive_has[None, :] & (arrive_slot[None, :] == slot_ids[:, None])
    matched = jnp.concatenate([own_match, in_match], axis=1)
    source = jnp.sum(
        jnp.where(matched, jnp.arange(stored + size_gy, dtype=jnp.int32)[None, :], 0), axis=1
    )
    filled = jnp.any(matched, axis=1)
    root_scale = math.sqrt(devices * SLOTS * TILE)
    received = lax.all_to_all(
        jnp.where(send_has[:, None, None], tile_stack[send_index], jnp.zeros((), tile_stack.dtype)),
        "gy",
        split_axis=0,
        concat_axis=0,
        tiled=True,
    )
    combined = jnp.concatenate([tile_stack, received], axis=0)
    balanced = jnp.where(
        filled[:, None, None], combined[source], jnp.zeros((), tile_stack.dtype)
    ).reshape(-1, breadth)
    low_factor = factor(balanced)
    ortho_rows = normalise(low_factor, balanced, root_scale)
    return (ortho_rows, low_factor.T / root_scale)


def solution(mesh):
    placed = (P(("gx", "gy"), None), P("gx"), P("gx", None))
    return jax.shard_map(
        on_device,
        mesh=mesh,
        in_specs=placed,
        out_specs=(P(("gx", "gy"), None), P()),
        check_vma=False,
    )
```

profile of v0, /device:TPU:1, one launch (start us, length us, event | category | flops | bytes accessed | tf_op | source)
XLA Modules:
  0.0 738.9 jit_solution(11730234620089552840)
XLA Ops:
  9.2 7.4 %gather_fusion = bf16[16,128,1024]{2,1,0:T(8,128)(2,1)} fusion(bf16[48,128,1024]{2,1,0:T(8,128)(2,1)} %bitcast.133, s32[1024]{0:T(1024)S(1)} %pad_clamp_fusion.1), kind=kCustom, calls=%fused_computation | custom fusion | bytes 8388672 | tf_op jit(solution)/shard_map/gather | solution.py:62
  21.2 8.5 %all-to-all-start = ((bf16[16,128,1024]{2,1,0:T(8,128)(2,1)}), bf16[16,128,1024]{2,1,0:T(8,128)(2,1)}, u32[]{:S(2)}, u32[]{:S(2)}) async-start(bf16[16,128,1024]{2,1,0:T(8,128)(2,1)} %broadcast_select_fusion), calls=%async_computation | async-start | bytes 8388608 | tf_op jit(solution)/shard_map/all_to_all | solution.py:61
  30.1 62.0 %all-to-all-done = bf16[16,128,1024]{2,1,0:T(8,128)(2,1)} async-done(((bf16[16,128,1024]{2,1,0:T(8,128)(2,1)}), bf16[16,128,1024]{2,1,0:T(8,128)(2,1)}, u32[]{:S(2)}, u32[]{:S(2)}) %all-to-all-start) | async-done | bytes 4194336 | tf_op jit(solution)/shard_map/all_to_all | solution.py:61
  92.1 13.8 %pad_maximum_fusion = bf16[64,128,1024]{2,1,0:T(8,128)(2,1)} fusion(bf16[16,128,1024]{2,1,0:T(8,128)(2,1)} %all-to-all-done, bf16[48,128,1024]{2,1,0:T(8,128)(2,1)} %bitcast.134), kind=kLoop, calls=%fused_computation.4 | loop fusion | flops 8388608 | bytes 33554432 | tf_op jit(solution)/shard_map/concatenate | solution.py:68
  105.9 10.9 %gather_fusion.1 = bf16[32,128,1024]{2,1,0:T(8,128)(2,1)} fusion(bf16[64,128,1024]{2,1,0:T(8,128)(2,1)} %pad_maximum_fusion, s32[1024]{0:T(1024)S(1)} %pad_clamp_fusion), kind=kCustom, calls=%fused_computation.1 | custom fusion | bytes 16777344 | tf_op jit(solution)/shard_map/gather | solution.py:70
  116.9 15.6 %fusion.30 = f32[1024,1024]{0,1:T(8,128)} fusion(bf16[32,128,1024]{2,1,0:T(8,128)(2,1)} %gather_fusion.1, pred[32]{0:T(512)(128)(4,1)S(1)} %reduce_or.41), kind=kOutput, calls=%fused_computation.44 | convolution fusion | flops 8594128896 | bytes 12582944 | tf_op jit(solution)/shard_map/dot_general | solution.py:13
  132.6 11.3 %copy.19 = bf16[4096,1024]{0,1:T(8,128)(2,1)} copy(bf16[4096,1024]{1,0:T(8,128)(2,1)} %bitcast.132) | data formatting | bytes 16777216 | tf_op jit(solution)/shard_map/gather | solution.py:70
  143.9 11.6 %fusion.90 = (f32[1024,4096]{1,0:T(8,128)}, bf16[1024,4096]{1,0:T(8,128)(2,1)}) fusion(bf16[4096,1024]{0,1:T(8,128)(2,1)} %copy.19, pred[4096]{0:T(1024)(128)(4,1)S(1)} %broadcast_bitcast_fusion), kind=kLoop, calls=%fused_computation.208 | loop fusion | flops 8388608 | bytes 33558528 | tf_op jit(solution)/shard_map/transpose | solution.py:22
  155.5 131.8 %all-reduce.3.cloned.1.call-done = f32[1024,1024]{0,1:T(8,128)} async-done(((f32[1024,1024]{0,1:T(8,128)}), f32[1024,1024]{0,1:T(8,128)}) %all-reduce.3.cloned.1.call-update) | async-done | bytes 4194320 | tf_op jit(solution)/shard_map/psum | solution.py:16
  299.2 11.7 %cholesky.223 = f32[128,128]{1,0:T(8,128)S(1)} custom-call(f32[128,128]{1,0:T(8,128)S(1)} %cholesky.580), custom_call_target="Cholesky" | custom-call | tf_op jit(solution)/shard_map/jit(cholesky)/cholesky | solution.py:17
  311.7 9.8 %custom-call.63 = f32[1,128,128]{1,2,0:T(8,128)S(1)} custom-call(f32[1,128,128]{2,1,0:T(8,128)S(1)} %get-tuple-element.81), custom_call_target="InvertDiagBlocksLowerTriangular" | custom-call | tf_op jit(solution)/shard_map/jit(cholesky)/cholesky | solution.py:17
  327.9 12.2 %cholesky.244 = f32[128,128]{1,0:T(8,128)S(1)} custom-call(f32[128,128]{1,0:T(8,128)S(1)} %cholesky.584), custom_call_target="Cholesky" | custom-call | tf_op jit(solution)/shard_map/jit(cholesky)/cholesky | solution.py:17
  341.4 9.8 %custom-call.64 = f32[1,128,128]{1,2,0:T(8,128)S(1)} custom-call(f32[1,128,128]{2,1,0:T(8,128)S(1)} %get-tuple-element.78), custom_call_target="InvertDiagBlocksLowerTriangular" | custom-call | tf_op jit(solution)/shard_map/jit(cholesky)/cholesky | solution.py:17
  354.5 11.7 %cholesky.468 = f32[128,128]{1,0:T(8,128)S(1)} custom-call(f32[128,128]{1,0:T(8,128)S(1)} %cholesky.589), custom_call_target="Cholesky" | custom-call | tf_op jit(solution)/shard_map/jit(cholesky)/cholesky | solution.py:17
  367.5 9.8 %custom-call.65 = f32[1,128,128]{1,2,0:T(8,128)S(1)} custom-call(f32[1,128,128]{2,1,0:T(8,128)S(1)} %get-tuple-element.75), custom_call_target="InvertDiagBlocksLowerTriangular" | custom-call | tf_op jit(solution)/shard_map/jit(cholesky)/cholesky | solution.py:17
  380.8 11.8 %cholesky.487 = f32[128,128]{1,0:T(8,128)S(1)} custom-call(f32[128,128]{1,0:T(8,128)S(1)} %cholesky.594), custom_call_target="Cholesky" | custom-call | tf_op jit(solution)/shard_map/jit(cholesky)/cholesky | solution.py:17
  394.0 9.8 %custom-call.66 = f32[1,128,128]{1,2,0:T(8,128)S(1)} custom-call(f32[1,128,128]{2,1,0:T(8,128)S(1)} %get-tuple-element.72), custom_call_target="InvertDiagBlocksLowerTriangular" | custom-call | tf_op jit(solution)/shard_map/jit(cholesky)/cholesky | solution.py:17
  407.2 11.7 %cholesky.506 = f32[128,128]{1,0:T(8,128)S(1)} custom-call(f32[128,128]{1,0:T(8,128)S(1)} %cholesky.599), custom_call_target="Cholesky" | custom-call | tf_op jit(solution)/shard_map/jit(cholesky)/cholesky | solution.py:17
  420.3 10.0 %custom-call.67 = f32[1,128,128]{1,2,0:T(8,128)S(1)} custom-call(f32[1,128,128]{2,1,0:T(8,128)S(1)} %get-tuple-element.69), custom_call_target="InvertDiagBlocksLowerTriangular" | custom-call | tf_op jit(solution)/shard_map/jit(cholesky)/cholesky | solution.py:17
  433.6 11.7 %cholesky.526 = f32[128,128]{1,0:T(8,128)S(1)} custom-call(f32[128,128]{1,0:T(8,128)S(1)} %cholesky.604), custom_call_target="Cholesky" | custom-call | tf_op jit(solution)/shard_map/jit(cholesky)/cholesky | solution.py:17
  446.5 9.8 %custom-call.68 = f32[1,128,128]{1,2,0:T(8,128)S(1)} custom-call(f32[1,128,128]{2,1,0:T(8,128)S(1)} %get-tuple-element.66), custom_call_target="InvertDiagBlocksLowerTriangular" | custom-call | tf_op jit(solution)/shard_map/jit(cholesky)/cholesky | solution.py:17
  459.4 12.1 %cholesky.546 = f32[128,128]{1,0:T(8,128)S(1)} custom-call(f32[128,128]{1,0:T(8,128)S(1)} %cholesky.609), custom_call_target="Cholesky" | custom-call | tf_op jit(solution)/shard_map/jit(cholesky)/cholesky | solution.py:17
  472.7 9.8 %custom-call.69 = f32[1,128,128]{1,2,0:T(8,128)S(1)} custom-call(f32[1,128,128]{2,1,0:T(8,128)S(1)} %get-tuple-element.63), custom_call_target="InvertDiagBlocksLowerTriangular" | custom-call | tf_op jit(solution)/shard_map/jit(cholesky)/cholesky | solution.py:17
  485.3 11.7 %cholesky.564 = f32[128,128]{1,0:T(8,128)S(1)} custom-call(f32[128,128]{1,0:T(8,128)S(1)} %convolution_subtract_fusion.11), custom_call_target="Cholesky" | custom-call | tf_op jit(solution)/shard_map/jit(cholesky)/cholesky | solution.py:17
  503.1 6.7 multiply_bitcast_fusion
  515.2 23.4 %while.1 = (s32[]{:T(128)}, f32[1024,1024]{1,0:T(8,128)}, s32[8,2]{0,1:T(2,128)S(1)}, f32[8,128,128]{2,1,0:T(8,128)S(1)}, s32[]{:T(128)}) while((s32[]{:T(128)}, f32[1024,1024]{1,0:T(8,128)}, s32[8,2]{0,1:T(2,128)S(1)}, f32[8,128,128]{2,1,0:T(8,128)S(1)}, s32[]{:T(128)}) %tuple.73), condition=%wide.while_cond, body=%wide.while_body.sunk | while | flops 2 | bytes 131189 | solution.py:21
  538.6 78.8 %custom-call.70 = f32[8,128,128]{1,2,0:T(8,128)S(1)} custom-call(f32[8,128,128]{2,1,0:T(8,128)S(1)} %get-tuple-element.9), custom_call_target="InvertDiagBlocksLowerTriangular" | custom-call | tf_op jit(solution)/shard_map/jit(_solve_triangular)/triangular_solve | solution.py:21
  665.4 9.3 %convolution_subtract_fusion.1 = f32[128,4096]{1,0:T(8,128)S(1)} fusion(f32[640,4096]{1,0:T(8,128)} %get-tuple-element.43, f32[1024,4096]{1,0:T(8,128)S(1)} %bitcast.131, f32[1024,1024]{1,0:T(8,128)} %get-tuple-element.145), kind=kOutput, calls=%fused_computation.27 | convolution fusion | flops 4027056128 | bytes 15007744 | tf_op jit(solution)/shard_map/jit(_solve_triangular)/triangular_solve | solution.py:21
  680.3 9.8 %convolution_subtract_fusion = f32[128,4096]{1,0:T(8,128)S(1)} fusion(f32[768,4096]{1,0:T(8,128)} %get-tuple-element.39, f32[1024,4096]{1,0:T(8,128)S(1)} %bitcast.131, f32[1024,1024]{1,0:T(8,128)} %get-tuple-element.145), kind=kOutput, calls=%fused_computation.26 | convolution fusion | flops 4832362496 | bytes 17170432 | tf_op jit(solution)/shard_map/jit(_solve_triangular)/triangular_solve | solution.py:21
  694.9 11.7 %convolution_subtract_fusion.4 = f32[128,4096]{1,0:T(8,128)S(1)} fusion(f32[896,4096]{1,0:T(8,128)} %get-tuple-element.35, f32[1024,4096]{1,0:T(8,128)S(1)} %bitcast.131, f32[1024,1024]{1,0:T(8,128)} %get-tuple-element.145), kind=kOutput, calls=%fused_computation.30 | convolution fusion | flops 5637668864 | bytes 19333120 | tf_op jit(solution)/shard_map/jit(_solve_triangular)/triangular_solve | solution.py:21
  710.7 9.2 %fusion = bf16[4096,1024]{0,1:T(8,128)(2,1)} fusion(f32[1024,4096]{1,0:T(8,128)} %convolution_dynamic-update-slice_fusion), kind=kLoop, calls=%fused_computation.6 | loop fusion | flops 8388608 | bytes 25165824 | tf_op jit(solution)/shard_map/convert_element_type | solution.py:24
  719.9 11.9 %copy.20 = bf16[4096,1024]{1,0:T(8,128)(2,1)} copy(bf16[4096,1024]{0,1:T(8,128)(2,1)} %fusion) | data formatting | bytes 16777216
  (112 shorter events, 145.4 us)
Async XLA Ops:
  21.2 70.9 %all-to-all-start = ((bf16[16,128,1024]{2,1,0:T(8,128)(2,1)}), bf16[16,128,1024]{2,1,0:T(8,128)(2,1)}, u32[]{:S(2)}, u32[]{:S(2)}) async-start(bf16[16,128,1024]{2,1,0:T(8,128)(2,1)} %broadcast_select_fusion), calls=%async_computation | async-start | bytes 8388608 | tf_op jit(solution)/shard_map/all_to_all | solution.py:61
  29.6 257.6 %all-reduce.3.cloned.1.call-start = ((), (), s32[]{:S(2)}) async-start(), calls=%async_computation.1 | async-start | bytes 8388608 | tf_op jit(solution)/shard_map/psum | solution.py:16
  297.3 1.9 copy-start
  617.4 29.7 %copy-start.1 = (f32[8,128,128]{1,2,0:T(8,128)}, f32[8,128,128]{1,2,0:T(8,128)S(1)}, u32[]{:S(2)}) copy-start(f32[8,128,128]{1,2,0:T(8,128)S(1)} %custom-call.70) | copy-start | bytes 1572868
  617.4 15.6 %slice-start = ((s8[16777216]{0:T(1024)(128)(4,1)}), s8[4194304]{0:T(1024)(128)(4,1)S(1)}, s32[]{:S(2)}) async-start(s8[16777216]{0:T(1024)(128)(4,1)} %bitcast.130), calls=%async_computation.2 | async-start | bytes 8388608
  617.4 15.6 %slice-start.1 = ((s8[16777216]{0:T(1024)(128)(4,1)}), s8[4194304]{0:T(1024)(128)(4,1)S(1)}, s32[]{:S(2)}) async-start(s8[16777216]{0:T(1024)(128)(4,1)} %bitcast.130), calls=%async_computation.3 | async-start | bytes 8388608
  623.5 9.5 %slice-start.2 = ((s8[16777216]{0:T(1024)(128)(4,1)}), s8[4194304]{0:T(1024)(128)(4,1)S(1)}, s32[]{:S(2)}) async-start(s8[16777216]{0:T(1024)(128)(4,1)} %bitcast.130), calls=%async_computation.4 | async-start | bytes 8388608
  627.3 5.8 slice-start.3
Sparse Core Ops, SparseCore 0:
  132.6 154.5 all-reduce.2
where the time goes:
time: 747 us; the launch traced here: 739 us
  other arithmetic  305 us (41%)
  waiting for transfers between devices  194 us (26%)
  matrix products  132 us (18%)
  local copies, waits for them, and re-layouts  80.3 us (11%)
  between operations  19.5 us (3%)
  starting transfers between devices  8.51 us (1%)
    another operation x31, other arithmetic, factor(): return jnp.linalg.cholesky(summed)  173 us
    psum x1, waiting for transfers between devices, factor(): summed = lax.psum(gram_local, ('gx', 'gy'))  132 us
    another operation x15, matrix products, normalise(): jax.scipy.linalg.solve_triangular(low_factor, row_block.astype(jnp.float3...  93.2 us
    another operation x2, other arithmetic, normalise(): jax.scipy.linalg.solve_triangular(low_factor, row_block.astype(jnp.float3...  78.8 us
    all_to_all x1, waiting for transfers between devices, on_device(): lax.all_to_all(jnp.where(send_has[:, None, None], tile_stack[send_index],...  62 us
    another operation x24, local copies, waits for them, and re-layouts  23.3 us
    another operation x14, matrix products, factor(): return jnp.linalg.cholesky(summed)  23 us
    gather x2, local copies, waits for them, and re-layouts, on_device(): combined[source]  22.2 us
  transfers between devices with their start and end apart: 2, of which 2 were waited for; matrix products, arithmetic and copies ran while one was open for 3% of the time, Pallas kernels for 0%

commit v1 on v0

v1 whole, which is shorter than its diff:
```python
import math

import jax
import jax.numpy as jnp
from jax import lax
from jax.experimental import pallas as pl
from jax.experimental.pallas import tpu as pltpu
from jax.sharding import Mesh, PartitionSpec as P

TILE = 128
SLOTS = 32
W = 1024
NB = W // 128
MAX_LIVE = 44
CHUNK = 4
GROUP = 4
F32 = jnp.float32
BF16 = jnp.bfloat16
BLOCKS = [(i, j) for i in range(NB) for j in range(i, NB)]
HALF = len(BLOCKS) // 2
CHIPS = ("y", "z", "x")


def gram_kernel(heights_ref, x_ref, mine_ref, other_ref, acc_ref):
    step = pl.program_id(0)
    pos = lax.axis_index("z") * lax.axis_size("x") + lax.axis_index("x")
    core = lax.axis_index("core")
    live = heights_ref[pos]

    @pl.when(step == 0)
    def _():
        acc_ref[...] = jnp.zeros_like(acc_ref)

    def accumulate(x):
        for i in range(0, W, 256):
            acc_ref[i : i + 256, i:] += lax.dot_general(
                x[:, i : i + 256], x[:, i:], (((0,), (0,)), ((), ())), preferred_element_type=F32
            )

    @pl.when((step + 1) * CHUNK <= live)
    def _():
        accumulate(x_ref[...])

    @pl.when((step * CHUNK < live) & ((step + 1) * CHUNK > live))
    def _():
        rows = lax.broadcasted_iota(jnp.int32, x_ref.shape, 0)
        kept = rows < (live - step * CHUNK) * TILE
        accumulate(jnp.where(kept, x_ref[...].astype(F32), 0.0).astype(BF16))

    def put(ref, blocks):
        for b, (i, j) in enumerate(blocks):
            ref[b] = acc_ref[i * 128 : i * 128 + 128, j * 128 : j * 128 + 128]

    last = step == pl.num_programs(0) - 1

    @pl.when(last & (core == 0))
    def _():
        put(mine_ref, BLOCKS[:HALF])
        put(other_ref, BLOCKS[HALF:])

    @pl.when(last & (core == 1))
    def _():
        put(mine_ref, BLOCKS[HALF:])
        put(other_ref, BLOCKS[:HALF])


def gram(a_rows, heights):
    steps = -(-MAX_LIVE // CHUNK)

    def chunk_map(step, heights_ref):
        pos = lax.axis_index("z") * lax.axis_size("x") + lax.axis_index("x")
        return (jnp.minimum(step, lax.div(heights_ref[pos] + (CHUNK - 1), CHUNK) - 1), 0)

    whole = pl.BlockSpec((HALF, 128, 128), lambda step, heights_ref: (0, 0, 0))
    return pl.pallas_call(
        gram_kernel,
        grid_spec=pltpu.PrefetchScalarGridSpec(
            num_scalar_prefetch=1,
            grid=(steps,),
            in_specs=[pl.BlockSpec((CHUNK * TILE, W), chunk_map)],
            out_specs=[whole, whole],
            scratch_shapes=[pltpu.VMEM((W, W), F32)],
        ),
        out_shape=[jax.ShapeDtypeStruct((HALF, 128, 128), F32)] * 2,
        name="gram",
    )(heights, a_rows)


def pick_kernel(index_ref, a_ref, out_ref, buf_ref, in_sems, out_sems):
    count = out_ref.shape[0]
    loads = [
        pltpu.make_async_copy(a_ref.at[pl.ds(pl.multiple_of(index_ref[i] * TILE, TILE), TILE)], buf_ref.at[i], in_sems.at[i])
        for i in range(count)
    ]
    stores = [pltpu.make_async_copy(buf_ref.at[i], out_ref.at[i], out_sems.at[i]) for i in range(count)]
    for load in loads:
        load.start()
    for load, store in zip(loads, stores):
        load.wait()
        store.start()
    for store in stores:
        store.wait()


def pick_tiles(a_rows, index):
    count = index.shape[0]
    return pl.pallas_call(
        pick_kernel,
        grid_spec=pltpu.PrefetchScalarGridSpec(
            num_scalar_prefetch=1,
            grid=(),
            in_specs=[pl.BlockSpec(memory_space=pl.ANY)],
            out_specs=pl.BlockSpec(memory_space=pl.ANY),
            scratch_shapes=[
                pltpu.VMEM((count, TILE, W), BF16),
                pltpu.SemaphoreType.DMA((count,)),
                pltpu.SemaphoreType.DMA((count,)),
            ],
        ),
        out_shape=jax.ShapeDtypeStruct((count, TILE, W), BF16),
        name="pick",
    )(index, a_rows)


def lane_bcast(v, lane):
    return jnp.broadcast_to(v[:, lane : lane + 1], (8, 128))


def row_bcast(ref, p, s):
    return jnp.broadcast_to(ref[p, s : s + 1, :], (8, 128))


def factor_block(d_ref, rk_ref, dk_ref, es_ref, vs_ref, ws_ref):
    sub = lax.broadcasted_iota(jnp.int32, (8, 128), 0)
    lane = lax.broadcasted_iota(jnp.int32, (8, 128), 1)
    v = [d_ref[8 * g : 8 * g + 8, :] for g in range(16)]
    w = [jnp.where(lane == sub + 8 * g, 1.0, 0.0).astype(F32) for g in range(16)]

    def entries(q):
        for j in range(8):
            es_ref[8 * q + j] = lane_bcast(v[q], 8 * q + j)
        return {(i, j): row_bcast(es_ref, 8 * q + j, i) for j in range(8) for i in range(j, 8)}

    e = entries(0)
    for p in range(16):
        vs_ref[p] = v[p]
        ws_ref[p] = w[p]
        low, inv, rows, wide = {}, [], [], []
        for s in range(8):
            inv.append(lax.rsqrt(e[s, s]))
            for i in range(s + 1, 8):
                low[i, s] = e[i, s] * inv[s]
            for j in range(s + 1, 8):
                for i in range(j, 8):
                    e[i, j] = e[i, j] - low[i, s] * low[j, s]
            r, q = row_bcast(vs_ref, p, s), row_bcast(ws_ref, p, s)
            for t in range(s):
                r = r - low[s, t] * rows[t]
                q = q - low[s, t] * wide[t]
            rows.append(r * inv[s])
            wide.append(q * inv[s])
        for s in range(8):
            rk_ref[8 * p + s : 8 * p + s + 1, :] = rows[s][0:1]
            dk_ref[8 * p + s : 8 * p + s + 1, :] = wide[s][0:1]
        if p == 15:
            break
        e = entries(p + 1)
        spread = [[lane_bcast(rows[s], 8 * p + 8 + i) for i in range(8)] for s in range(8)]
        for s in range(8):
            for j in range(8):
                for i in range(j, 8):
                    e[i, j] = e[i, j] - spread[s][i] * spread[s][j]
        for g in range(p + 1, 16):
            for s in range(8):
                m = jnp.take_along_axis(rows[s], sub + 8 * g, axis=1, mode="promise_in_bounds")
                v[g] = v[g] - m * rows[s]
                w[g] = w[g] - m * wide[s]


def split3(x):
    h = x.astype(BF16)
    r = x - h.astype(F32)
    m = r.astype(BF16)
    return h, m, (r - m.astype(F32)).astype(BF16)


def put_left(ref, x):
    h, m, l = split3(x)
    ref[:, 0:128] = l
    ref[:, 128:256] = h
    ref[:, 256:384] = m
    ref[:, 384:512] = h


def put_right(ref, x):
    h, m, l = split3(x)
    ref[0:128] = m
    ref[128:256] = h
    ref[256:384] = l


def product(left_ref, right_ref):
    dot = lambda a, b: jnp.dot(a, b, preferred_element_type=F32)
    return (
        dot(left_ref[:, 0:256], right_ref[128:384])
        + dot(left_ref[:, 128:384], right_ref[0:256])
        + dot(left_ref[:, 256:512], right_ref[0:256])
    )


def chol_kernel(root, mine_ref, other_ref, hi_ref, lo_ref, r_ref, t_ref, d_ref, rk_ref, dk_ref, p_ref, left_ref, right_ref, es_ref, vs_ref, ws_ref):
    core = lax.axis_index("core")

    def take(ref, blocks):
        for b, (i, j) in enumerate(blocks):
            t_ref[i * 128 : i * 128 + 128, j * 128 : j * 128 + 128] = ref[b]

    @pl.when(core == 0)
    def _():
        take(mine_ref, BLOCKS[:HALF])
        take(other_ref, BLOCKS[HALF:])

    @pl.when(core == 1)
    def _():
        take(mine_ref, BLOCKS[HALF:])
        take(other_ref, BLOCKS[:HALF])

    sub = lax.broadcasted_iota(jnp.int32, (128, 128), 0)
    lane = lax.broadcasted_iota(jnp.int32, (128, 128), 1)
    wide_lane = lax.broadcasted_iota(jnp.int32, (128, W), 1)

    def block_row(k, carry):
        at = pl.multiple_of(k * 128, 128)
        here = pl.ds(at, 128)
        d_ref[...] = t_ref[here, here]
        factor_block(d_ref, rk_ref, dk_ref, es_ref, vs_ref, ws_ref)
        put_left(left_ref, dk_ref[...])
        put_right(right_ref, t_ref[here, :])
        p_ref[...] = product(left_ref, right_ref)
        r_ref[here, :] = jnp.where(wide_lane >= at + 128, p_ref[...] * (1.0 / root), 0.0)
        r_ref[here, here] = jnp.where(lane >= sub, rk_ref[...] * (1.0 / root), 0.0)
        p_ref[:, here] = dk_ref[...]
        scaled = jnp.where(wide_lane < at + 128, p_ref[...] * root, 0.0)
        hi = scaled.astype(BF16)
        hi_ref[here, :] = hi
        lo_ref[here, :] = (scaled - hi.astype(F32)).astype(BF16)
        put_right(right_ref, p_ref[...])

        def trailing(i, carry):
            below = pl.ds(pl.multiple_of(i * 128, 128), 128)
            put_left(left_ref, p_ref[:, below].T)
            t_ref[below, here] = jnp.zeros((128, 128), F32)
            t_ref[below, :] -= product(left_ref, right_ref)
            return carry

        lax.fori_loop(k + 1, NB, trailing, 0)
        return carry

    lax.fori_loop(0, NB, block_row, 0)


def cholesky(mine, other, root):
    return pl.pallas_call(
        lambda *refs: chol_kernel(root, *refs),
        out_shape=[
            jax.ShapeDtypeStruct((W, W), BF16),
            jax.ShapeDtypeStruct((W, W), BF16),
            jax.ShapeDtypeStruct((W, W), F32),
        ],
        scratch_shapes=[
            pltpu.VMEM((W, W), F32),
            pltpu.VMEM((128, 128), F32),
            pltpu.VMEM((128, 128), F32),
            pltpu.VMEM((128, 128), F32),
            pltpu.VMEM((128, W), F32),
            pltpu.VMEM((128, 512), BF16),
            pltpu.VMEM((384, W), BF16),
            pltpu.VMEM((128, 8, 128), F32),
            pltpu.VMEM((16, 8, 128), F32),
            pltpu.VMEM((16, 8, 128), F32),
        ],
        cost_estimate=pl.CostEstimate(flops=40_000_000_000, bytes_accessed=16_000_000, transcendentals=0),
        name="factor",
    )(mine, other)


def ortho_kernel(source_ref, filled_ref, a_ref, in_ref, hi_ref, lo_ref, out_ref, buf_ref, sems):
    step = pl.program_id(0)
    stored = a_ref.shape[0] // TILE

    def fetch(at, slot):
        for g in range(GROUP):
            src = source_ref[at * GROUP + g]
            dst = buf_ref.at[slot, pl.ds(g * TILE, TILE)]

            @pl.when(src < stored)
            def _():
                row = pl.multiple_of(src * TILE, TILE)
                pltpu.make_async_copy(a_ref.at[pl.ds(row, TILE)], dst, sems.at[slot, g]).start()

            @pl.when(src >= stored)
            def _():
                pltpu.make_async_copy(in_ref.at[src - stored], dst, sems.at[slot, g]).start()

    slot = lax.rem(step, 2)

    @pl.when(step == 0)
    def _():
        fetch(0, 0)

    @pl.when(step + 1 < pl.num_programs(0))
    def _():
        fetch(step + 1, 1 - slot)

    for g in range(GROUP):
        here = buf_ref.at[slot, pl.ds(g * TILE, TILE)]
        pltpu.make_async_copy(a_ref.at[pl.ds(0, TILE)], here, sems.at[slot, g]).wait()

        @pl.when(filled_ref[step * GROUP + g] == 0)
        def _():
            here[...] = jnp.zeros((TILE, W), BF16)

    nt = (((1,), (1,)), ((), ()))
    for j in range(0, W, 256):
        x = buf_ref[slot, :, : j + 256]
        acc = lax.dot_general(x, hi_ref[j : j + 256, : j + 256], nt, preferred_element_type=F32)
        acc += lax.dot_general(x, lo_ref[j : j + 256, : j + 256], nt, preferred_element_type=F32)
        out_ref[:, j : j + 256] = acc.astype(BF16)


def ortho(a_rows, received, source, filled, hi, lo):
    rows = GROUP * TILE
    square = pl.BlockSpec((W, W), lambda step, *_: (0, 0))
    return pl.pallas_call(
        ortho_kernel,
        grid_spec=pltpu.PrefetchScalarGridSpec(
            num_scalar_prefetch=2,
            grid=(SLOTS // GROUP,),
            in_specs=[pl.BlockSpec(memory_space=pl.ANY), pl.BlockSpec(memory_space=pl.ANY), square, square],
            out_specs=pl.BlockSpec((rows, W), lambda step, *_: (step, 0)),
            scratch_shapes=[pltpu.VMEM((2, rows, W), BF16), pltpu.SemaphoreType.DMA((2, GROUP))],
        ),
        out_shape=jax.ShapeDtypeStruct((SLOTS * TILE, W), BF16),
        name="ortho",
    )(source, filled, a_rows, received, hi, lo)


def plan(heights, destination):
    size_gy = lax.axis_size("z") * lax.axis_size("x")
    group_pos = lax.axis_index("z") * lax.axis_size("x") + lax.axis_index("x")
    group_base = (lax.axis_index("y") * lax.axis_size("core") + lax.axis_index("core")) * size_gy
    my_index = group_base + group_pos
    stored = destination.shape[1]
    tile_ids = jnp.arange(stored, dtype=jnp.int32)
    peer_ids = jnp.arange(size_gy, dtype=jnp.int32)
    slot_ids = jnp.arange(SLOTS, dtype=jnp.int32)
    tile_live = tile_ids[None, :] < heights[:, None]
    target_dev = destination // SLOTS
    target_slot = destination % SLOTS
    own_live = tile_live[group_pos]
    own_dev = target_dev[group_pos]
    own_slot = target_slot[group_pos]
    leaving = own_live & (own_dev != my_index)
    chosen = leaving[None, :] & (own_dev[None, :] - group_base == peer_ids[:, None])
    send_index = jnp.sum(jnp.where(chosen, tile_ids[None, :], 0), axis=1)
    arriving = tile_live & (target_dev == my_index) & (peer_ids[:, None] != group_pos)
    arrive_slot = jnp.sum(jnp.where(arriving, target_slot, 0), axis=1)
    arrive_has = jnp.any(arriving, axis=1)
    staying = own_live & (own_dev == my_index)
    own_match = staying[None, :] & (own_slot[None, :] == slot_ids[:, None])
    in_match = arrive_has[None, :] & (arrive_slot[None, :] == slot_ids[:, None])
    matched = jnp.concatenate([own_match, in_match], axis=1)
    places = jnp.arange(stored + size_gy, dtype=jnp.int32)
    source = jnp.sum(jnp.where(matched, places[None, :], 0), axis=1)
    filled = jnp.any(matched, axis=1).astype(jnp.int32)
    return send_index, source, filled


def swap_core(x):
    return lax.ppermute(x, "core", [(0, 1), (1, 0)])


def exchange(x, axes):
    return lax.all_to_all(x, axes, split_axis=0, concat_axis=0, tiled=True)


def on_device(a_rows, heights, destination):
    chips = math.prod(lax.axis_size(name) for name in CHIPS)
    root = math.sqrt(chips * 2 * SLOTS * TILE)
    mine, other = gram(a_rows, heights)
    half = (mine + swap_core(other)).reshape(chips, -1, 128)
    shard = jnp.sum(exchange(half, CHIPS), axis=0)
    send_index, source, filled = plan(heights, destination)
    tiles = pick_tiles(a_rows, send_index)
    full = exchange(jnp.broadcast_to(shard[None], half.shape), CHIPS)
    tiles, full = lax.optimization_barrier((tiles, full))
    mine = full.reshape(HALF, 128, 128)
    other = swap_core(mine)
    received = exchange(tiles, ("z", "x"))
    hi, lo, factor_r = cholesky(mine, other, root)
    ortho_rows = ortho(a_rows, received, source, filled, hi, lo)
    return (ortho_rows, factor_r)


def solution(mesh):
    fine = Mesh(mesh.devices.reshape(4, 2, 4, 4), ("y", "core", "z", "x"))
    every = ("y", "core", "z", "x")
    return jax.shard_map(
        on_device,
        mesh=fine,
        in_specs=(P(every, None), P(("y", "core")), P(("y", "core"), None)),
        out_specs=(P(every, None), P()),
        check_vma=False,
    )
```

time: 747 us -> 172 us (0.23)
  other arithmetic: 305 us -> 4.1 us
  waiting for transfers between devices: 194 us -> 19.4 us
  matrix products: 132 us -> 0 us
  Pallas kernels: 0 us -> 89.1 us
  local copies, waits for them, and re-layouts: 80.3 us -> 2.42 us
  blocking collectives: 0 us -> 41.5 us
  between operations: 19.5 us -> 0.89 us
    another operation x33 -> x0, other arithmetic: 252 us -> none  [the longest x31 173 us: factor(): return jnp.linalg.cholesky(summed)]
    psum x1 -> x0, waiting for transfers between devices: 132 us -> none  [factor(): summed = lax.psum(gram_local, ('gx', 'gy'))]
    another operation x29 -> x0, matrix products: 116 us -> none  [the longest x15 93.2 us: normalise(): jax.scipy.linalg.solve_triangular(low_factor, row_block.astype(jnp.float3...]
    pallas_call x0 -> x4, Pallas kernels: none -> 89.1 us  [the longest x1 57.8 us: cholesky(): pl.pallas_call(lambda *refs: chol_kernel(root, *refs), out_shape=[jax.Sha...]
    all_to_all x1 -> x2, waiting for transfers between devices: 62 us -> 16.7 us  [exchange(): return lax.all_to_all(x, axes, split_axis=0, concat_axis=0, tiled=True)]
    all_to_all x0 -> x1, blocking collectives: none -> 41.5 us  [exchange(): return lax.all_to_all(x, axes, split_axis=0, concat_axis=0, tiled=True)]
    gather x3 -> x0, local copies, waits for them, and re-layouts: 29.6 us -> none  [the longest x2 22.2 us: on_device(): combined[source]]
    another operation x33 -> x0, local copies, waits for them, and re-layouts: 25.9 us -> none
  transfers between devices with their start and end apart: 2 -> 4, of which waited for: 2 -> 3; matrix products, arithmetic and copies ran while one was open for 3% -> 2% of each run, Pallas kernels for 0% -> 38%
where the time goes in v1:
time: 172 us; the launch traced here: 171 us
  Pallas kernels  89.1 us (52%)
  blocking collectives  41.5 us (24%)
  waiting for transfers between devices  19.4 us (11%)
  starting transfers between devices  13.6 us (8%)
  other arithmetic  4.1 us (2%)
  local copies, waits for them, and re-layouts  2.42 us (1%)
    pallas_call x1, Pallas kernels, cholesky(): pl.pallas_call(lambda *refs: chol_kernel(root, *refs), out_shape=[jax.Sha...  57.8 us
    all_to_all x1, blocking collectives, exchange(): return lax.all_to_all(x, axes, split_axis=0, concat_axis=0, tiled=True)  41.5 us
    pallas_call x1, Pallas kernels, ortho(): pl.pallas_call(ortho_kernel, grid_spec=pltpu.PrefetchScalarGridSpec(num_s...  18.8 us
    all_to_all x2, waiting for transfers between devices, exchange(): return lax.all_to_all(x, axes, split_axis=0, concat_axis=0, tiled=True)  16.7 us
    all_to_all x2, starting transfers between devices, exchange(): return lax.all_to_all(x, axes, split_axis=0, concat_axis=0, tiled=True)  9.33 us
    pallas_call x1, Pallas kernels, pick_tiles(): pl.pallas_call(pick_kernel, grid_spec=pltpu.PrefetchScalarGridSpec(num_sc...  7.01 us
    pallas_call x1, Pallas kernels, gram(): pl.pallas_call(gram_kernel, grid_spec=pltpu.PrefetchScalarGridSpec(num_sc...  5.46 us
    ppermute x2, starting transfers between devices, swap_core(): return lax.ppermute(x, 'core', [(0, 1), (1, 0)])  4.29 us
  transfers between devices with their start and end apart: 4, of which 3 were waited for; matrix products, arithmetic and copies ran while one was open for 2% of the time, Pallas kernels for 38%

profile of v1, /device:TPU:1, one launch (start us, length us, event | category | flops | bytes accessed | tf_op | source)
XLA Modules:
  0.0 171.1 jit_solution(13995649206072324633)
XLA Ops:
  0.6 5.5 %gram.1 = (f32[18,128,128]{2,1,0:T(8,128)}, f32[18,128,128]{2,1,0:T(8,128)}) custom-call(s32[16]{0:T(128)} %heights_ref.1, bf16[6144,1024]{1,0:T(8,128)(2,1)} %a_ref.3), custom_call_target="tpu_custom_call" | custom-call | tf_op jit(solution)/shard_map/gram/pallas_call | solution.py:75
  6.1 1.3 collective-permute-start
  7.4 2.7 %collective-permute-done = f32[18,128,128]{2,1,0:T(8,128)S(1)} collective-permute-done((f32[18,128,128]{2,1,0:T(8,128)}, f32[18,128,128]{2,1,0:T(8,128)S(1)}, u32[]{:S(2)}, u32[]{:S(2)}) %collective-permute-start) | collective-permute-done | bytes 1179680 | tf_op jit(solution)/shard_map/ppermute | solution.py:380
  10.1 1.4 add.29
  11.5 0.1 reshape.19
  11.6 41.5 %all_to_all.15 = f32[64,36,128]{2,1,0:T(8,128)S(1)} all-to-all(f32[64,36,128]{2,1,0:T(8,128)S(1)} %reshape.19), channel_id=1, replica_groups=mesh['y'=4,'core'=2,'z'=4,'x'=4] {'y','z','x'}, dimensions={0} | all-to-all | bytes 2359296 | tf_op jit(solution)/shard_map/all_to_all | solution.py:384
  53.2 0.1 reduce_sum.39
  53.3 1.1 broadcast_in_dim.22
  54.4 0.0 copy-start.1
  54.4 4.8 %all-to-all-start.1 = ((f32[64,36,128]{2,1,0:T(8,128)}), f32[64,36,128]{2,1,0:T(8,128)S(1)}, u32[]{:S(2)}, u32[]{:S(2)}) async-start(f32[64,36,128]{2,1,0:T(8,128)} %broadcast_in_dim.22), calls=%async_computation.1 | async-start | bytes 2621440 | tf_op jit(solution)/shard_map/all_to_all | solution.py:384
  59.3 0.0 copy-done.1
  59.3 0.0 copy-done.2
  59.3 0.2 fusion.8
  59.5 0.1 select_reduce_fusion.2
  59.6 0.7 select_reduce_fusion.1.index_ref
  60.3 7.0 %pick.1 = bf16[16,128,1024]{2,1,0:T(8,128)(2,1)} custom-call(s32[16]{0:T(128)} %select_reduce_fusion.1.index_ref, bf16[6144,1024]{1,0:T(8,128)(2,1)} %a_ref.3), custom_call_target="tpu_custom_call" | custom-call | tf_op jit(solution)/shard_map/pick/pallas_call | solution.py:107
  67.4 11.7 %all-to-all-done.1 = f32[64,36,128]{2,1,0:T(8,128)S(1)} async-done(((f32[64,36,128]{2,1,0:T(8,128)}), f32[64,36,128]{2,1,0:T(8,128)S(1)}, u32[]{:S(2)}, u32[]{:S(2)}) %all-to-all-start.1) | async-done | bytes 1179680 | tf_op jit(solution)/shard_map/all_to_all | solution.py:384
  79.0 0.1 reshape.20.refs_0_
  79.1 0.0 copy-start
  79.1 2.9 %collective-permute-start.1 = (f32[18,128,128]{2,1,0:T(8,128)S(1)}, f32[18,128,128]{2,1,0:T(8,128)S(1)}, u32[]{:S(2)}, u32[]{:S(2)}) collective-permute-start(f32[18,128,128]{2,1,0:T(8,128)S(1)} %reshape.20.refs_0_), channel_id=1, source_target_pairs={{0,16},{16,0},{1,17},{17,1},{2,18},{18,2},{3,19},{19,3},{4,20},{20... | collective-permute-start | bytes 3538952 | tf_op jit(solution)/shard_map/ppermute | solution.py:380
  82.1 0.1 fusion.6
  82.2 0.1 copy.5
  82.3 0.1 fusion.7
  82.4 0.7 select_reduce_fusion.source_ref
  83.1 0.0 copy-done
  83.1 4.5 %all-to-all-start.2 = ((bf16[16,128,1024]{2,1,0:T(8,128)(2,1)}), bf16[16,128,1024]{2,1,0:T(8,128)(2,1)}, u32[]{:S(2)}, u32[]{:S(2)}) async-start(bf16[16,128,1024]{2,1,0:T(8,128)(2,1)} %pick.1), calls=%async_computation.2 | async-start | bytes 8388608 | tf_op jit(solution)/shard_map/all_to_all | solution.py:384
  87.7 0.6 or_convert_fusion.filled_ref
  88.3 0.0 collective-permute-done.1.refs_1_
  88.3 1.0 copy-done.3
  89.3 57.8 %factor.1 = (bf16[1024,1024]{1,0:T(8,128)(2,1)}, bf16[1024,1024]{1,0:T(8,128)(2,1)}, f32[1024,1024]{1,0:T(8,128)}) custom-call(f32[18,128,128]{2,1,0:T(8,128)} %copy-done, f32[18,128,128]{2,1,0:T(8,128)} %copy-done.3), custom_call_target="tpu_custom_call" | custom-call | flops 40000000000 | bytes 16000000 | tf_op jit(solution)/shard_map/factor/pallas_call | solution.py:263
  147.1 5.0 %all-to-all-done.2.in_ref = bf16[16,128,1024]{2,1,0:T(8,128)(2,1)} async-done(((bf16[16,128,1024]{2,1,0:T(8,128)(2,1)}), bf16[16,128,1024]{2,1,0:T(8,128)(2,1)}, u32[]{:S(2)}, u32[]{:S(2)}) %all-to-all-start.2) | async-done | bytes 4194336 | tf_op jit(solution)/shard_map/all_to_all | solution.py:384
  152.1 18.8 %ortho.1 = bf16[4096,1024]{1,0:T(8,128)(2,1)} custom-call(s32[32]{0:T(128)} %select_reduce_fusion.source_ref, s32[32]{0:T(128)} %or_convert_fusion.filled_ref, bf16[6144,1024]{1,0:T(8,128)(2,1)} %a_ref.3, bf16[16,128,1024]{2,1,0:T(8,128)(2,1)} %all-to-all-done.2.in_ref, bf16[1024,1024]{1,0:T(8,128)(2,1)} %get-tuple-element.13.hi_ref, ...), custom_call_target="tpu_custom_call" | custom-call | tf_op jit(solution)/shard_map/ortho/pallas_call | solution.py:334
  (5 shorter events, 0.0 us)
Async XLA Ops:
  6.1 4.0 %collective-permute-start = (f32[18,128,128]{2,1,0:T(8,128)}, f32[18,128,128]{2,1,0:T(8,128)S(1)}, u32[]{:S(2)}, u32[]{:S(2)}) collective-permute-start(f32[18,128,128]{2,1,0:T(8,128)} %get-tuple-element.10), channel_id=1, source_target_pairs={{0,16},{16,0},{1,17},{17,1},{2,18},{18,2},{3,19},{19,3},{4,20},{20... | collective-permute-start | bytes 3538952 | tf_op jit(solution)/shard_map/ppermute | solution.py:380
  54.4 4.8 %copy-start.1 = (s32[16,48]{1,0:T(8,128)S(1)}, s32[16,48]{1,0:T(8,128)}, u32[]{:S(2)}) copy-start(s32[16,48]{1,0:T(8,128)} %param.5) | copy-start | bytes 9220
  54.4 4.8 %copy-start.2 = (s32[16]{0:T(128)S(1)}, s32[16]{0:T(128)}, u32[]{:S(2)}) copy-start(s32[16]{0:T(128)} %heights_ref.1) | copy-start | bytes 196
  54.4 24.6 %all-to-all-start.1 = ((f32[64,36,128]{2,1,0:T(8,128)}), f32[64,36,128]{2,1,0:T(8,128)S(1)}, u32[]{:S(2)}, u32[]{:S(2)}) async-start(f32[64,36,128]{2,1,0:T(8,128)} %broadcast_in_dim.22), calls=%async_computation.1 | async-start | bytes 2621440 | tf_op jit(solution)/shard_map/all_to_all | solution.py:384
  79.1 4.0 %copy-start = (f32[18,128,128]{2,1,0:T(8,128)}, f32[18,128,128]{2,1,0:T(8,128)S(1)}, u32[]{:S(2)}) copy-start(f32[18,128,128]{2,1,0:T(8,128)S(1)} %reshape.20.refs_0_) | copy-start | bytes 3538948
  79.1 9.1 %collective-permute-start.1 = (f32[18,128,128]{2,1,0:T(8,128)S(1)}, f32[18,128,128]{2,1,0:T(8,128)S(1)}, u32[]{:S(2)}, u32[]{:S(2)}) collective-permute-start(f32[18,128,128]{2,1,0:T(8,128)S(1)} %reshape.20.refs_0_), channel_id=1, source_target_pairs={{0,16},{16,0},{1,17},{17,1},{2,18},{18,2},{3,19},{19,3},{4,20},{20... | collective-permute-start | bytes 3538952 | tf_op jit(solution)/shard_map/ppermute | solution.py:380
  83.1 69.0 %all-to-all-start.2 = ((bf16[16,128,1024]{2,1,0:T(8,128)(2,1)}), bf16[16,128,1024]{2,1,0:T(8,128)(2,1)}, u32[]{:S(2)}, u32[]{:S(2)}) async-start(bf16[16,128,1024]{2,1,0:T(8,128)(2,1)} %pick.1), calls=%async_computation.2 | async-start | bytes 8388608 | tf_op jit(solution)/shard_map/all_to_all | solution.py:384
  88.3 1.0 copy-start.3

commit v2 on v1

v2 whole, which is shorter than its diff:
```python
import math

import jax
import jax.numpy as jnp
from jax import lax
from jax.experimental import pallas as pl
from jax.experimental.pallas import tpu as pltpu
from jax.sharding import Mesh, PartitionSpec as P


TILE = 128
SLOTS = 32
W = 1024
NB = W // 128
CHUNK = 4
GROUP = 8
DEEP = 4
F32 = jnp.float32
BF16 = jnp.bfloat16
BLOCKS = [(i, j) for i in range(NB) for j in range(i, NB)]
HALF = len(BLOCKS) // 2
CHIPS = ("y", "z", "x")


def gram_kernel(heights_ref, a_ref, mine_ref, other_ref, acc_ref, buf_ref, sems):
    core = lax.axis_index("core")
    live = heights_ref[lax.axis_index("z") * lax.axis_size("x") + lax.axis_index("x")]
    count = lax.div(live + (CHUNK - 1), CHUNK)
    rows = CHUNK * TILE

    def load(at):
        slot = lax.rem(at, DEEP)
        first = pl.multiple_of(at * rows, rows)
        return pltpu.make_async_copy(a_ref.at[pl.ds(first, rows)], buf_ref.at[slot], sems.at[slot])

    for early in range(DEEP - 1):

        @pl.when(early < count)
        def _():
            load(early).start()

    acc_ref[...] = jnp.zeros_like(acc_ref)

    def accumulate(x):
        flipped = x.T
        for j in range(0, W, 256):
            acc_ref[: j + 256, j : j + 256] += jnp.dot(
                flipped[: j + 256], x[:, j : j + 256], preferred_element_type=F32
            )

    def chunk(at, carry):
        @pl.when(at + DEEP - 1 < count)
        def _():
            load(at + DEEP - 1).start()

        load(at).wait()
        here = buf_ref.at[lax.rem(at, DEEP)]

        @pl.when((at + 1) * CHUNK > live)
        def _():
            kept = lax.broadcasted_iota(jnp.int32, (rows, W), 0) < (live - at * CHUNK) * TILE
            here[...] = jnp.where(kept, here[...].astype(F32), 0.0).astype(BF16)

        accumulate(here[...])
        return carry

    lax.fori_loop(0, count, chunk, 0)

    def put(ref, blocks):
        for b, (i, j) in enumerate(blocks):
            ref[b] = acc_ref[i * 128 : i * 128 + 128, j * 128 : j * 128 + 128]

    @pl.when(core == 0)
    def _():
        put(mine_ref, BLOCKS[:HALF])
        put(other_ref, BLOCKS[HALF:])

    @pl.when(core == 1)
    def _():
        put(mine_ref, BLOCKS[HALF:])
        put(other_ref, BLOCKS[:HALF])


def gram(a_rows, heights):
    return pl.pallas_call(
        gram_kernel,
        in_specs=[pl.BlockSpec(memory_space=pltpu.SMEM), pl.BlockSpec(memory_space=pltpu.HBM)],
        out_specs=[pl.BlockSpec(memory_space=pltpu.VMEM)] * 2,
        scratch_shapes=[
            pltpu.VMEM((W, W), F32),
            pltpu.VMEM((DEEP, CHUNK * TILE, W), BF16),
            pltpu.SemaphoreType.DMA((DEEP,)),
        ],
        out_shape=[jax.ShapeDtypeStruct((HALF, 128, 128), F32)] * 2,
        compiler_params=pltpu.CompilerParams(vmem_limit_bytes=52 * 1024 * 1024),
        name="gram",
    )(heights, a_rows)


def pick_kernel(index_ref, a_ref, *refs):
    outs, (buf_ref, in_sems, out_sems) = refs[:-3], refs[-3:]
    count = len(outs)
    loads = [
        pltpu.make_async_copy(a_ref.at[pl.ds(pl.multiple_of(index_ref[i] * TILE, TILE), TILE)], buf_ref.at[i], in_sems.at[i])
        for i in range(count)
    ]
    stores = [pltpu.make_async_copy(buf_ref.at[i], outs[i], out_sems.at[i]) for i in range(count)]
    for load in loads:
        load.start()
    for load, store in zip(loads, stores):
        load.wait()
        store.start()
    for store in stores:
        store.wait()


def pick_tiles(a_rows, index):
    count = index.shape[0]
    return pl.pallas_call(
        pick_kernel,
        in_specs=[pl.BlockSpec(memory_space=pltpu.SMEM), pl.BlockSpec(memory_space=pltpu.HBM)],
        out_specs=[pl.BlockSpec(memory_space=pltpu.HBM)] * count,
        scratch_shapes=[
            pltpu.VMEM((count, TILE, W), BF16),
            pltpu.SemaphoreType.DMA((count,)),
            pltpu.SemaphoreType.DMA((count,)),
        ],
        out_shape=[jax.ShapeDtypeStruct((TILE, W), BF16)] * count,
        compiler_params=pltpu.CompilerParams(vmem_limit_bytes=56 * 1024 * 1024),
        name="pick",
    )(index, a_rows)


def lane_bcast(v, lane):
    return jnp.broadcast_to(v[:, lane : lane + 1], (8, 128))


def row_bcast(ref, p, s):
    return jnp.broadcast_to(ref[p, s : s + 1, :], (8, 128))


def factor_block(d_ref, rk_ref, dk_ref, es_ref, ms_ref, vs_ref):
    sub = lax.broadcasted_iota(jnp.int32, (8, 128), 0)
    lane = lax.broadcasted_iota(jnp.int32, (8, 128), 1)
    v = [d_ref[8 * g : 8 * g + 8, :] for g in range(16)]
    columns = [lane_bcast(v[0], j) for j in range(8)]
    for p in range(16):
        for j in range(8):
            es_ref[8 * p + j] = columns[j]
        vs_ref[p] = v[p]
        e = {(i, j): row_bcast(es_ref, 8 * p + j, i) for j in range(8) for i in range(j, 8)}
        inside = (lane >= 8 * p) & (lane < 8 * p + 8)
        low, inv, rows, wide, both = {}, [], [], [], []
        for s in range(8):
            inv.append(lax.rsqrt(e[s, s]))
            for i in range(s + 1, 8):
                low[i, s] = e[i, s] * inv[s]
            for j in range(s + 1, 8):
                for i in range(j, 8):
                    e[i, j] = e[i, j] - low[i, s] * low[j, s]
            r, q = row_bcast(vs_ref, p, s), jnp.where(lane == 8 * p + s, 1.0, 0.0).astype(F32)
            for t in range(s):
                r = r - low[s, t] * rows[t]
                q = q - low[s, t] * wide[t]
            rows.append(r * inv[s])
            wide.append(q * inv[s])
            both.append(jnp.where(inside, wide[s], rows[s]))
            rk_ref[8 * p + s : 8 * p + s + 1, :] = rows[s][0:1]
            dk_ref[8 * p + s : 8 * p + s + 1, :] = both[s][0:1]
        if p == 15:
            break
        after = 8 * p + 8
        columns = [lane_bcast(v[p + 1], after + j) for j in range(8)]
        for s in range(8):
            m = jnp.take_along_axis(rows[s], sub + after, axis=1, mode="promise_in_bounds")
            ms_ref[8 * p + s] = m
            for j in range(8):
                columns[j] = columns[j] - m * row_bcast(ms_ref, 8 * p + s, j)
        for g in range(p + 1, 16):
            v[g] = jnp.where(inside, 0.0, v[g])
            for s in range(8):
                m = jnp.take_along_axis(rows[s], sub + 8 * g, axis=1, mode="promise_in_bounds")
                v[g] = v[g] - m * both[s]


PASSES = 6
LEFT, RIGHT = ("mhh", "hmh") if PASSES == 3 else ("lhhmmh", "hlmhmh")


def split(x):
    h = x.astype(BF16)
    r = x - h.astype(F32)
    m = r.astype(BF16)
    return {"h": h, "m": m, "l": (r - m.astype(F32)).astype(BF16) if PASSES > 3 else None}


def put_left(ref, x):
    parts = split(x)
    for at, name in enumerate(LEFT):
        ref[:, at * 128 : at * 128 + 128] = parts[name]


def put_right(ref, x):
    parts = split(x)
    for at, name in enumerate(RIGHT):
        ref[at * 128 : at * 128 + 128] = parts[name]


def product(left_ref, right_ref):
    return jnp.dot(left_ref[...], right_ref[...], preferred_element_type=F32)


def chol_kernel(root, mine_ref, other_ref, hi_ref, lo_ref, r_ref, t_ref, d_ref, rk_ref, dk_ref, p_ref, left_ref, right_ref, es_ref, ms_ref, vs_ref, hi_out, lo_out, r_out, in_sems, out_sems):
    core = lax.axis_index("core")

    def block_copy(ref, b, at):
        i, j = BLOCKS[at]
        return pltpu.make_async_copy(
            ref.at[b], t_ref.at[i * 128 : i * 128 + 128, j * 128 : j * 128 + 128], in_sems.at[at]
        )

    for owner in range(2):

        @pl.when(core == owner)
        def _():
            for b in range(HALF):
                block_copy(mine_ref, b, owner * HALF + b).start()
            for b in range(HALF):
                block_copy(other_ref, b, (1 - owner) * HALF + b).start()

    def arrived(first, last):
        for at in range(first, last):
            block_copy(mine_ref, 0, at).wait()

    arrived(0, NB)
    sub = lax.broadcasted_iota(jnp.int32, (128, 128), 0)
    lane = lax.broadcasted_iota(jnp.int32, (128, 128), 1)
    wide_lane = lax.broadcasted_iota(jnp.int32, (128, W), 1)

    def leave(k):
        slot = lax.rem(k, 2)
        here = pl.ds(pl.multiple_of(k * 128, 128), 128)
        return [
            pltpu.make_async_copy(stage.at[slot], out.at[here], out_sems.at[n, slot])
            for n, (stage, out) in enumerate(((hi_out, hi_ref), (lo_out, lo_ref), (r_out, r_ref)))
        ]

    def block_row(k, carry):
        at = pl.multiple_of(k * 128, 128)
        here = pl.ds(at, 128)
        slot = lax.rem(k, 2)
        d_ref[...] = t_ref[here, here]
        factor_block(d_ref, rk_ref, dk_ref, es_ref, ms_ref, vs_ref)
        dk_ref[...] = jnp.where(lane <= sub, dk_ref[...], 0.0)
        put_left(left_ref.at[0:128], dk_ref[...])
        put_right(right_ref, t_ref[here, :])
        p_ref[...] = product(left_ref.at[0:128], right_ref)

        @pl.when(k >= 2)
        def _():
            for copy in leave(k - 2):
                copy.wait()

        r_out[slot] = jnp.where(wide_lane >= at + 128, p_ref[...] * (1.0 / root), 0.0)
        r_out[slot, :, here] = jnp.where(lane >= sub, rk_ref[...] * (1.0 / root), 0.0)
        p_ref[:, here] = dk_ref[...]
        scaled = jnp.where(wide_lane < at + 128, p_ref[...] * root, 0.0)
        hi = scaled.astype(BF16)
        hi_out[slot] = hi
        lo_out[slot] = (scaled - hi.astype(F32)).astype(BF16)
        for copy in leave(k):
            copy.start()

        @pl.when(k == 0)
        def _():
            arrived(NB, 2 * HALF)

        put_right(right_ref, p_ref[...])

        def trailing(first):
            put_left(left_ref.at[first:W], p_ref[:, first:].T)
            t_ref[first:, here] = jnp.zeros((W - first, 128), F32)
            for j in range(0, W, 256):
                t_ref[first:, j : j + 256] -= product(left_ref.at[first:W], right_ref.at[:, j : j + 256])

        for first in range(0, W, 256):
            pl.when((lax.div(k + 1, 2) * 256 == first) & (k < NB - 1))(lambda first=first: trailing(first))

        return carry

    lax.fori_loop(0, NB, block_row, 0)
    for k in (NB - 2, NB - 1):
        for copy in leave(k):
            copy.wait()


def cholesky(mine, other, root):
    hbm = pl.BlockSpec(memory_space=pltpu.HBM)
    return pl.pallas_call(
        lambda *refs: chol_kernel(root, *refs),
        out_shape=[
            jax.ShapeDtypeStruct((W, W), BF16),
            jax.ShapeDtypeStruct((W, W), BF16),
            jax.ShapeDtypeStruct((W, W), F32),
        ],
        in_specs=[hbm] * 2,
        out_specs=[hbm] * 3,
        scratch_shapes=[
            pltpu.VMEM((W, W), F32),
            pltpu.VMEM((128, 128), F32),
            pltpu.VMEM((128, 128), F32),
            pltpu.VMEM((128, 128), F32),
            pltpu.VMEM((128, W), F32),
            pltpu.VMEM((W, 128 * PASSES), BF16),
            pltpu.VMEM((128 * PASSES, W), BF16),
            pltpu.VMEM((128, 8, 128), F32),
            pltpu.VMEM((128, 8, 128), F32),
            pltpu.VMEM((16, 8, 128), F32),
            pltpu.VMEM((2, 128, W), BF16),
            pltpu.VMEM((2, 128, W), BF16),
            pltpu.VMEM((2, 128, W), F32),
            pltpu.SemaphoreType.DMA((2 * HALF,)),
            pltpu.SemaphoreType.DMA((3, 2)),
        ],
        cost_estimate=pl.CostEstimate(flops=40_000_000_000, bytes_accessed=16_000_000, transcendentals=0),
        compiler_params=pltpu.CompilerParams(vmem_limit_bytes=50 * 1024 * 1024),
        name="factor",
    )(mine, other)


def ortho_kernel(own_ref, arrive_ref, a_ref, hi_hbm, lo_hbm, *refs):
    came, (out_ref, buf_ref, hi_ref, lo_ref, sems, w_sems) = refs[:-6], refs[-6:]
    step = pl.program_id(0)

    def fetch(src, slot):
        return pltpu.make_async_copy(src, buf_ref.at[pl.ds(pl.multiple_of(slot * TILE, TILE), TILE)], sems.at[slot])

    def weights(j):
        part = (pl.ds(j, 256), pl.ds(0, j + 256))
        return [
            pltpu.make_async_copy(src.at[part], dst.at[part], w_sems.at[n, j // 256])
            for n, (src, dst) in enumerate(((hi_hbm, hi_ref), (lo_hbm, lo_ref)))
        ]

    @pl.when(step == 0)
    def _():
        for j in range(0, W, 256):
            for copy in weights(j):
                copy.start()

        def own(slot, carry):
            tile = own_ref[slot]

            @pl.when(tile >= 0)
            def _():
                fetch(a_ref.at[pl.ds(pl.multiple_of(tile * TILE, TILE), TILE)], slot).start()

            return carry

        lax.fori_loop(0, SLOTS, own, 0)
        for n, ref in enumerate(came):
            slot = arrive_ref[n]

            @pl.when(slot >= 0)
            def _():
                fetch(ref, slot).start()

    for g in range(GROUP):
        slot = step * GROUP + g
        full = own_ref[slot] >= 0
        for n in range(len(came)):
            full |= arrive_ref[n] == slot

        @pl.when(full)
        def _():
            fetch(a_ref.at[pl.ds(0, TILE)], slot).wait()

        @pl.when(jnp.logical_not(full))
        def _():
            buf_ref[pl.ds(pl.multiple_of(slot * TILE, TILE), TILE)] = jnp.zeros((TILE, W), BF16)

    @pl.when(step == 0)
    def _():
        for j in range(0, W, 256):
            for copy in weights(j):
                copy.wait()

    nt = (((1,), (1,)), ((), ()))
    rows = pl.ds(pl.multiple_of(step * (GROUP * TILE), GROUP * TILE), GROUP * TILE)
    for j in range(0, W, 256):
        x = buf_ref[rows, : j + 256]
        acc = lax.dot_general(x, hi_ref[j : j + 256, : j + 256], nt, preferred_element_type=F32)
        acc += lax.dot_general(x, lo_ref[j : j + 256, : j + 256], nt, preferred_element_type=F32)
        out_ref[:, j : j + 256] = acc.astype(BF16)


def ortho(a_rows, received, own, arrive, hi, lo):
    return pl.pallas_call(
        ortho_kernel,
        grid_spec=pltpu.PrefetchScalarGridSpec(
            num_scalar_prefetch=2,
            grid=(SLOTS // GROUP,),
            in_specs=[pl.BlockSpec(memory_space=pltpu.HBM)] * (3 + len(received)),
            out_specs=pl.BlockSpec((GROUP * TILE, W), lambda step, *_: (step, 0)),
            scratch_shapes=[
                pltpu.VMEM((SLOTS * TILE, W), BF16),
                pltpu.VMEM((W, W), BF16),
                pltpu.VMEM((W, W), BF16),
                pltpu.SemaphoreType.DMA((SLOTS,)),
                pltpu.SemaphoreType.DMA((2, W // 256)),
            ],
        ),
        out_shape=jax.ShapeDtypeStruct((SLOTS * TILE, W), BF16),
        compiler_params=pltpu.CompilerParams(vmem_limit_bytes=50 * 1024 * 1024),
        name="ortho",
    )(own, arrive, a_rows, hi, lo, *received)


def shift(pos, dz, dx):
    size_z, size_x = lax.axis_size("z"), lax.axis_size("x")
    return (pos // size_x + dz) % size_z * size_x + (pos % size_x + dx) % size_x


def shifts():
    pairs = [(dz, dx) for dz in range(lax.axis_size("z")) for dx in range(lax.axis_size("x"))]
    return pairs[1:]


def plan(heights, destination):
    size_gy = lax.axis_size("z") * lax.axis_size("x")
    group_pos = lax.axis_index("z") * lax.axis_size("x") + lax.axis_index("x")
    group_base = (lax.axis_index("y") * lax.axis_size("core") + lax.axis_index("core")) * size_gy
    my_index = group_base + group_pos
    tile_ids = jnp.arange(destination.shape[1], dtype=jnp.int32)
    peers = jnp.arange(size_gy, dtype=jnp.int32)
    slot_ids = jnp.arange(SLOTS, dtype=jnp.int32)
    moves = jnp.array(shifts(), jnp.int32)
    to = shift(group_pos, moves[:, 0], moves[:, 1])
    source = shift(group_pos, -moves[:, 0], -moves[:, 1])
    mine = peers == group_pos
    own_live = tile_ids < jnp.sum(jnp.where(mine, heights, 0))
    own_dest = jnp.sum(jnp.where(mine[:, None], destination, 0), axis=0)
    chosen = own_live[None, :] & ((own_dest // SLOTS)[None, :] == (group_base + to)[:, None])
    send_index = jnp.sum(jnp.where(chosen, tile_ids[None, :], 0), axis=1)
    landed = own_live[None, :] & (own_dest[None, :] == (my_index * SLOTS + slot_ids)[:, None])
    arriving = (tile_ids[None, :] < heights[:, None]) & (destination // SLOTS == my_index)
    by_peer = jnp.sum(jnp.where(arriving, destination % SLOTS + 1, 0), axis=1) - 1
    own = jnp.sum(jnp.where(landed, tile_ids[None, :] + 1, 0), axis=1) - 1
    arrive = jnp.sum(jnp.where(source[:, None] == peers[None, :], by_peer[None, :], 0), axis=1)
    return send_index, own, arrive


def swap_core(x):
    return lax.ppermute(x, "core", [(0, 1), (1, 0)])


def exchange(x, axes):
    return lax.all_to_all(x, axes, split_axis=0, concat_axis=0, tiled=True)


def on_device(a_rows, heights, destination):
    chips = math.prod(lax.axis_size(name) for name in CHIPS)
    root = math.sqrt(chips * 2 * SLOTS * TILE)
    mine, other = gram(a_rows, heights)
    half = (mine + swap_core(other)).reshape(chips, -1, 128)
    parts = exchange(half, CHIPS)
    send_index, own, arrive = plan(heights, destination)
    tiles = pick_tiles(a_rows, send_index)
    shard = jnp.sum(parts, axis=0)
    full = exchange(jnp.broadcast_to(shard[None], half.shape), CHIPS)
    size_gy = lax.axis_size("z") * lax.axis_size("x")
    received = [
        lax.ppermute(tile, ("z", "x"), [(i, shift(i, *move)) for i in range(size_gy)])
        for tile, move in zip(tiles, shifts())
    ]
    mine = full.reshape(HALF, 128, 128)
    other = swap_core(mine)
    hi, lo, factor_r = cholesky(mine, other, root)
    ortho_rows = ortho(a_rows, received, own, arrive, hi, lo)
    return (ortho_rows, factor_r)


def solution(mesh):
    fine = Mesh(mesh.devices.reshape(4, 2, 4, 4), ("y", "core", "z", "x"))
    every = ("y", "core", "z", "x")
    return jax.shard_map(
        on_device,
        mesh=fine,
        in_specs=(P(every, None), P(("y", "core")), P(("y", "core"), None)),
        out_specs=(P(every, None), P()),
        check_vma=False,
    )
```

time: 172 us -> 209 us (1.22)
  starting transfers between devices: 13.6 us -> 45.8 us
  waiting for transfers between devices: 19.4 us -> 48.1 us
  Pallas kernels: 89.1 us -> 75 us
  blocking collectives: 41.5 us -> 32.9 us
    ppermute x0 -> x15, starting transfers between devices: none -> 38.2 us  [on_device(): lax.ppermute(tile, ('z', 'x'), [(i, shift(i, *move)) for i in range(size_...]
    ppermute x0 -> x15, waiting for transfers between devices: none -> 26.7 us  [on_device(): lax.ppermute(tile, ('z', 'x'), [(i, shift(i, *move)) for i in range(size_...]
    pallas_call x1, Pallas kernels: 57.8 us -> 40 us  [cholesky(): pl.pallas_call(lambda *refs: chol_kernel(root, *refs), out_shape=[jax.Sha...]
    all_to_all x1, blocking collectives: 41.5 us -> 32.9 us  [exchange(): return lax.all_to_all(x, axes, split_axis=0, concat_axis=0, tiled=True)]
    pallas_call x2, Pallas kernels: 12.5 us -> 18.2 us  [the longest x1 13.1 us: gram(): pl.pallas_call(gram_kernel, in_specs=[pl.BlockSpec(memory_space=pltpu.SME...]
    all_to_all x2 -> x1, starting transfers between devices: 9.33 us -> 4.81 us  [exchange(): return lax.all_to_all(x, axes, split_axis=0, concat_axis=0, tiled=True)]
    all_to_all x2 -> x1, waiting for transfers between devices: 16.7 us -> 18.4 us  [exchange(): return lax.all_to_all(x, axes, split_axis=0, concat_axis=0, tiled=True)]
  transfers between devices with their start and end apart: 4 -> 18, of which waited for: 3 -> 5; matrix products, arithmetic and copies ran while one was open for 2% -> 1% of each run, Pallas kernels for 38% -> 22%
where the time goes in v2:
time: 209 us; the launch traced here: 208 us
  Pallas kernels  75 us (36%)
  waiting for transfers between devices  48.1 us (23%)
  starting transfers between devices  45.8 us (22%)
  blocking collectives  32.9 us (16%)
  other arithmetic  2.9 us (1%)
    pallas_call x1, Pallas kernels, cholesky(): pl.pallas_call(lambda *refs: chol_kernel(root, *refs), out_shape=[jax.Sha...  40 us
    ppermute x15, starting transfers between devices, on_device(): lax.ppermute(tile, ('z', 'x'), [(i, shift(i, *move)) for i in range(size_...  38.2 us
    all_to_all x1, blocking collectives, exchange(): return lax.all_to_all(x, axes, split_axis=0, concat_axis=0, tiled=True)  32.9 us
    ppermute x15, waiting for transfers between devices, on_device(): lax.ppermute(tile, ('z', 'x'), [(i, shift(i, *move)) for i in range(size_...  26.7 us
    all_to_all x1, waiting for transfers between devices, exchange(): return lax.all_to_all(x, axes, split_axis=0, concat_axis=0, tiled=True)  18.4 us
    pallas_call x1, Pallas kernels, ortho(): pl.pallas_call(ortho_kernel, grid_spec=pltpu.PrefetchScalarGridSpec(num_s...  16.8 us
    pallas_call x1, Pallas kernels, gram(): pl.pallas_call(gram_kernel, in_specs=[pl.BlockSpec(memory_space=pltpu.SME...  13.1 us
    pallas_call x1, Pallas kernels, pick_tiles(): pl.pallas_call(pick_kernel, in_specs=[pl.BlockSpec(memory_space=pltpu.SME...  5.06 us
  transfers between devices with their start and end apart: 18, of which 5 were waited for; matrix products, arithmetic and copies ran while one was open for 1% of the time, Pallas kernels for 22%

profile of v2, /device:TPU:1, one launch (start us, length us, event | category | flops | bytes accessed | tf_op | source)
XLA Modules:
  0.0 207.8 jit_solution(14631477518643281669)
XLA Ops:
  0.6 0.6 copy-done
  1.3 13.1 %gram.1 = (f32[18,128,128]{2,1,0:T(8,128)S(1)}, f32[18,128,128]{2,1,0:T(8,128)}) custom-call(s32[16]{0:T(128)S(1)} %copy-done, bf16[6144,1024]{1,0:T(8,128)(2,1)} %a_ref.5), custom_call_target="tpu_custom_call" | custom-call | tf_op jit(solution)/shard_map/gram/pallas_call | solution.py:85
  14.5 3.0 %collective-permute-done = f32[18,128,128]{2,1,0:T(8,128)S(1)} collective-permute-done((f32[18,128,128]{2,1,0:T(8,128)}, f32[18,128,128]{2,1,0:T(8,128)S(1)}, u32[]{:S(2)}, u32[]{:S(2)}) %collective-permute-start) | collective-permute-done | bytes 1179680 | tf_op jit(solution)/shard_map/ppermute | solution.py:454
  17.5 0.2 add.139
  17.8 32.9 %all_to_all.10 = f32[64,36,128]{2,1,0:T(8,128)S(1)} all-to-all(f32[64,36,128]{2,1,0:T(8,128)S(1)} %reshape.50), channel_id=1, replica_groups=mesh['y'=4,'core'=2,'z'=4,'x'=4] {'y','z','x'}, dimensions={0} | all-to-all | bytes 2359296 | tf_op jit(solution)/shard_map/all_to_all | solution.py:458
  50.8 1.1 broadcast_in_dim.81
  51.9 4.8 %all-to-all-start.1 = ((f32[64,36,128]{2,1,0:T(8,128)}), f32[64,36,128]{2,1,0:T(8,128)S(1)}, u32[]{:S(2)}, u32[]{:S(2)}) async-start(f32[64,36,128]{2,1,0:T(8,128)} %broadcast_in_dim.81), calls=%async_computation.1 | async-start | bytes 2621440 | tf_op jit(solution)/shard_map/all_to_all | solution.py:458
  56.8 0.6 select_reduce_fusion.4
  57.4 0.6 iota_compare_fusion.3
  58.1 0.2 fusion.3
  58.3 18.4 %all-to-all-done.1 = f32[64,36,128]{2,1,0:T(8,128)S(1)} async-done(((f32[64,36,128]{2,1,0:T(8,128)}), f32[64,36,128]{2,1,0:T(8,128)S(1)}, u32[]{:S(2)}, u32[]{:S(2)}) %all-to-all-start.1) | async-done | bytes 1179680 | tf_op jit(solution)/shard_map/all_to_all | solution.py:458
  76.8 2.8 %collective-permute-start.1 = (f32[18,128,128]{2,1,0:T(8,128)S(1)}, f32[18,128,128]{2,1,0:T(8,128)S(1)}, u32[]{:S(2)}, u32[]{:S(2)}) collective-permute-start(f32[18,128,128]{2,1,0:T(8,128)S(1)} %reshape.51.refs_0_), channel_id=1, source_target_pairs={{0,16},{16,0},{1,17},{17,1},{2,18},{18,2},{3,19},{19,3},{4,20},{20... | collective-permute-start | bytes 3538952 | tf_op jit(solution)/shard_map/ppermute | solution.py:454
  79.6 0.7 select_reduce_fusion.1.index_ref
  80.3 5.1 %pick.1 = (bf16[128,1024]{1,0:T(8,128)(2,1)}, bf16[128,1024]{1,0:T(8,128)(2,1)}, bf16[128,1024]{1,0:T(8,128)(2,1)}, bf16[128,1024]{1,0:T(8,128)(2,1)}, bf16[128,...) custom-call(s32[15]{0:T(128)} %select_reduce_fusion.1.index_ref, ...), custom_call_target="tpu_custom_call" | custom-call | tf_op jit(solution)/shard_map/pick/pallas_call | solution.py:119
  85.4 2.0 collective-permute-start.2
  87.4 1.5 collective-permute-start.3
  88.9 1.3 collective-permute-start.4
  90.3 3.5 %collective-permute-done.2.refs_0_ = bf16[128,1024]{1,0:T(8,128)(2,1)S(1)} collective-permute-done((bf16[128,1024]{1,0:T(8,128)(2,1)}, bf16[128,1024]{1,0:T(8,128)(2,1)S(1)}, u32[]{:S(2)}, u32[]{:S(2)}) %collective-permute-start.2) | collective-permute-done | bytes 262176 | tf_op jit(solution)/shard_map/ppermute | solution.py:473
  93.8 1.6 collective-permute-start.6
  95.5 5.8 %collective-permute-done.3.refs_1_ = bf16[128,1024]{1,0:T(8,128)(2,1)S(1)} collective-permute-done((bf16[128,1024]{1,0:T(8,128)(2,1)}, bf16[128,1024]{1,0:T(8,128)(2,1)S(1)}, u32[]{:S(2)}, u32[]{:S(2)}) %collective-permute-start.3) | collective-permute-done | bytes 262176 | tf_op jit(solution)/shard_map/ppermute | solution.py:473
  101.2 1.4 collective-permute-start.7
  102.6 0.2 select_reduce_fusion
  102.9 2.1 %collective-permute-start.8 = (bf16[128,1024]{1,0:T(8,128)(2,1)}, bf16[128,1024]{1,0:T(8,128)(2,1)S(1)}, u32[]{:S(2)}, u32[]{:S(2)}) collective-permute-start(bf16[128,1024]{1,0:T(8,128)(2,1)} %get-tuple-element.32), channel_id=1, source_target_pairs={{0,7},{1,4},{2,5},{3,6},{4,11},{5,8},{6,9},{7,10},{8,15},{9,12},{1... | collective-permute-start | bytes 786440 | tf_op jit(solution)/shard_map/ppermute | solution.py:473
  105.0 1.3 collective-permute-start.9
  106.3 12.4 %collective-permute-start.10 = (bf16[128,1024]{1,0:T(8,128)(2,1)}, bf16[128,1024]{1,0:T(8,128)(2,1)S(1)}, u32[]{:S(2)}, u32[]{:S(2)}) collective-permute-start(bf16[128,1024]{1,0:T(8,128)(2,1)} %get-tuple-element.34), channel_id=1, source_target_pairs={{0,9},{1,10},{2,11},{3,8},{4,13},{5,14},{6,15},{7,12},{8,1},{9,2},... | collective-permute-start | bytes 786440 | tf_op jit(solution)/shard_map/ppermute | solution.py:473
  118.7 9.3 %collective-permute-start.11 = (bf16[128,1024]{1,0:T(8,128)(2,1)}, bf16[128,1024]{1,0:T(8,128)(2,1)S(1)}, u32[]{:S(2)}, u32[]{:S(2)}) collective-permute-start(bf16[128,1024]{1,0:T(8,128)(2,1)} %get-tuple-element.35), channel_id=1, source_target_pairs={{0,10},{1,11},{2,8},{3,9},{4,14},{5,15},{6,12},{7,13},{8,2},{9,3},... | collective-permute-start | bytes 786440 | tf_op jit(solution)/shard_map/ppermute | solution.py:473
  128.1 0.2 select_reduce_fusion.2.arrive_ref
  128.3 17.4 %collective-permute-done.9.refs_7_ = bf16[128,1024]{1,0:T(8,128)(2,1)S(1)} collective-permute-done((bf16[128,1024]{1,0:T(8,128)(2,1)}, bf16[128,1024]{1,0:T(8,128)(2,1)S(1)}, u32[]{:S(2)}, u32[]{:S(2)}) %collective-permute-start.9) | collective-permute-done | bytes 262176 | tf_op jit(solution)/shard_map/ppermute | solution.py:473
  145.8 2.9 %collective-permute-start.15 = (bf16[128,1024]{1,0:T(8,128)(2,1)}, bf16[128,1024]{1,0:T(8,128)(2,1)S(1)}, u32[]{:S(2)}, u32[]{:S(2)}) collective-permute-start(bf16[128,1024]{1,0:T(8,128)(2,1)} %get-tuple-element.39), channel_id=1, source_target_pairs={{0,14},{1,15},{2,12},{3,13},{4,2},{5,3},{6,0},{7,1},{8,6},{9,7},{1... | collective-permute-start | bytes 786440 | tf_op jit(solution)/shard_map/ppermute | solution.py:473
  148.7 2.0 collective-permute-start.16
  150.7 40.0 %factor.1 = (bf16[1024,1024]{1,0:T(8,128)(2,1)}, bf16[1024,1024]{1,0:T(8,128)(2,1)}, f32[1024,1024]{1,0:T(8,128)}) custom-call(f32[18,128,128]{2,1,0:T(8,128)S(1)} %reshape.51.refs_0_, f32[18,128,128]{2,1,0:T(8,128)S(1)} %collective-permute-done.1.refs_1_), custom_call_target="tpu_custom_call" | custom-call | flops 40000000000 | bytes 16000000 | tf_op jit(solution)/shard_map/factor/pallas_call | solution.py:299
  190.8 16.8 %ortho.1 = bf16[4096,1024]{1,0:T(8,128)(2,1)} custom-call(s32[32]{0:T(128)S(1)} %broadcast_add_fusion.1.own_ref, s32[15]{0:T(128)S(1)} %select_reduce_fusion.2.arrive_ref, bf16[6144,1024]{1,0:T(8,128)(2,1)} %a_ref.5, bf16[1024,1024]{1,0:T(8,128)(2,1)} %get-tuple-element.24.hi_hbm, bf16[1024,1024]{1,0:T(8,128)(2,1)} %get-tuple-element.25.lo_hbm, ...), custom_call_target="tpu_custom_call" | custom-call | tf_op jit(solution)/shard_map/ortho/pallas_call | solution.py:398
  (42 shorter events, 0.6 us)
Async XLA Ops:
  0.6 0.7 copy-start
  14.4 3.1 %collective-permute-start = (f32[18,128,128]{2,1,0:T(8,128)}, f32[18,128,128]{2,1,0:T(8,128)S(1)}, u32[]{:S(2)}, u32[]{:S(2)}) collective-permute-start(f32[18,128,128]{2,1,0:T(8,128)} %get-tuple-element.23), channel_id=1, source_target_pairs={{0,16},{16,0},{1,17},{17,1},{2,18},{18,2},{3,19},{19,3},{4,20},{20... | collective-permute-start | bytes 3538952 | tf_op jit(solution)/shard_map/ppermute | solution.py:454
  51.9 4.9 %copy-start.1 = (s32[16]{0:T(128)S(1)}, s32[16]{0:T(128)}, u32[]{:S(2)}) copy-start(s32[16]{0:T(128)} %heights_ref.1) | copy-start | bytes 196
  51.9 6.2 %copy-start.2 = (s32[16,48]{1,0:T(8,128)S(1)}, s32[16,48]{1,0:T(8,128)}, u32[]{:S(2)}) copy-start(s32[16,48]{1,0:T(8,128)} %param.6) | copy-start | bytes 9220
  51.9 6.4 %copy-start.5 = (s32[15,1]{0,1:T(1,128)S(1)}, s32[15,1]{0,1:T(1,128)}, u32[]{:S(2)}) copy-start(s32[15,1]{0,1:T(1,128)} %constant.122) | copy-start | bytes 184
  51.9 6.4 %copy-start.6 = (s32[15,1]{0,1:T(1,128)S(1)}, s32[15,1]{0,1:T(1,128)}, u32[]{:S(2)}) copy-start(s32[15,1]{0,1:T(1,128)} %constant.120) | copy-start | bytes 184
  51.9 24.8 %all-to-all-start.1 = ((f32[64,36,128]{2,1,0:T(8,128)}), f32[64,36,128]{2,1,0:T(8,128)S(1)}, u32[]{:S(2)}, u32[]{:S(2)}) async-start(f32[64,36,128]{2,1,0:T(8,128)} %broadcast_in_dim.81), calls=%async_computation.1 | async-start | bytes 2621440 | tf_op jit(solution)/shard_map/all_to_all | solution.py:458
  76.8 71.9 %collective-permute-start.1 = (f32[18,128,128]{2,1,0:T(8,128)S(1)}, f32[18,128,128]{2,1,0:T(8,128)S(1)}, u32[]{:S(2)}, u32[]{:S(2)}) collective-permute-start(f32[18,128,128]{2,1,0:T(8,128)S(1)} %reshape.51.refs_0_), channel_id=1, source_target_pairs={{0,16},{16,0},{1,17},{17,1},{2,18},{18,2},{3,19},{19,3},{4,20},{20... | collective-permute-start | bytes 3538952 | tf_op jit(solution)/shard_map/ppermute | solution.py:454
  80.3 22.5 %copy-start.3 = (s32[15,1]{0,1:T(1,128)S(1)}, s32[15,1]{0,1:T(1,128)}, u32[]{:S(2)}) copy-start(s32[15,1]{0,1:T(1,128)} %constant.123) | copy-start | bytes 184
  80.3 22.5 %copy-start.4 = (s32[15,1]{0,1:T(1,128)S(1)}, s32[15,1]{0,1:T(1,128)}, u32[]{:S(2)}) copy-start(s32[15,1]{0,1:T(1,128)} %constant.121) | copy-start | bytes 184
  85.4 8.4 %collective-permute-start.2 = (bf16[128,1024]{1,0:T(8,128)(2,1)}, bf16[128,1024]{1,0:T(8,128)(2,1)S(1)}, u32[]{:S(2)}, u32[]{:S(2)}) collective-permute-start(bf16[128,1024]{1,0:T(8,128)(2,1)} %get-tuple-element.26), channel_id=1, source_target_pairs={{0,1},{1,2},{2,3},{3,0},{4,5},{5,6},{6,7},{7,4},{8,9},{9,10},{10,1... | collective-permute-start | bytes 786440 | tf_op jit(solution)/shard_map/ppermute | solution.py:473
  87.4 13.8 %collective-permute-start.3 = (bf16[128,1024]{1,0:T(8,128)(2,1)}, bf16[128,1024]{1,0:T(8,128)(2,1)S(1)}, u32[]{:S(2)}, u32[]{:S(2)}) collective-permute-start(bf16[128,1024]{1,0:T(8,128)(2,1)} %get-tuple-element.27), channel_id=1, source_target_pairs={{0,2},{1,3},{2,0},{3,1},{4,6},{5,7},{6,4},{7,5},{8,10},{9,11},{10,... | collective-permute-start | bytes 786440 | tf_op jit(solution)/shard_map/ppermute | solution.py:473
  88.9 14.0 %collective-permute-start.4 = (bf16[128,1024]{1,0:T(8,128)(2,1)}, bf16[128,1024]{1,0:T(8,128)(2,1)S(1)}, u32[]{:S(2)}, u32[]{:S(2)}) collective-permute-start(bf16[128,1024]{1,0:T(8,128)(2,1)} %get-tuple-element.28), channel_id=1, source_target_pairs={{0,3},{1,0},{2,1},{3,2},{4,7},{5,4},{6,5},{7,6},{8,11},{9,8},{10,9... | collective-permute-start | bytes 786440 | tf_op jit(solution)/shard_map/ppermute | solution.py:473
  90.2 14.8 %collective-permute-start.5 = (bf16[128,1024]{1,0:T(8,128)(2,1)}, bf16[128,1024]{1,0:T(8,128)(2,1)S(1)}, u32[]{:S(2)}, u32[]{:S(2)}) collective-permute-start(bf16[128,1024]{1,0:T(8,128)(2,1)} %get-tuple-element.29), channel_id=1, source_target_pairs={{0,4},{1,5},{2,6},{3,7},{4,8},{5,9},{6,10},{7,11},{8,12},{9,13},{1... | collective-permute-start | bytes 786440 | tf_op jit(solution)/shard_map/ppermute | solution.py:473
  93.8 12.5 %collective-permute-start.6 = (bf16[128,1024]{1,0:T(8,128)(2,1)}, bf16[128,1024]{1,0:T(8,128)(2,1)S(1)}, u32[]{:S(2)}, u32[]{:S(2)}) collective-permute-start(bf16[128,1024]{1,0:T(8,128)(2,1)} %get-tuple-element.30), channel_id=1, source_target_pairs={{0,5},{1,6},{2,7},{3,4},{4,9},{5,10},{6,11},{7,8},{8,13},{9,14},{1... | collective-permute-start | bytes 786440 | tf_op jit(solution)/shard_map/ppermute | solution.py:473
  101.2 17.5 %collective-permute-start.7 = (bf16[128,1024]{1,0:T(8,128)(2,1)}, bf16[128,1024]{1,0:T(8,128)(2,1)S(1)}, u32[]{:S(2)}, u32[]{:S(2)}) collective-permute-start(bf16[128,1024]{1,0:T(8,128)(2,1)} %get-tuple-element.31), channel_id=1, source_target_pairs={{0,6},{1,7},{2,4},{3,5},{4,10},{5,11},{6,8},{7,9},{8,14},{9,15},{1... | collective-permute-start | bytes 786440 | tf_op jit(solution)/shard_map/ppermute | solution.py:473
  102.9 25.4 %collective-permute-start.8 = (bf16[128,1024]{1,0:T(8,128)(2,1)}, bf16[128,1024]{1,0:T(8,128)(2,1)S(1)}, u32[]{:S(2)}, u32[]{:S(2)}) collective-permute-start(bf16[128,1024]{1,0:T(8,128)(2,1)} %get-tuple-element.32), channel_id=1, source_target_pairs={{0,7},{1,4},{2,5},{3,6},{4,11},{5,8},{6,9},{7,10},{8,15},{9,12},{1... | collective-permute-start | bytes 786440 | tf_op jit(solution)/shard_map/ppermute | solution.py:473
  105.0 40.8 %collective-permute-start.9 = (bf16[128,1024]{1,0:T(8,128)(2,1)}, bf16[128,1024]{1,0:T(8,128)(2,1)S(1)}, u32[]{:S(2)}, u32[]{:S(2)}) collective-permute-start(bf16[128,1024]{1,0:T(8,128)(2,1)} %get-tuple-element.33), channel_id=1, source_target_pairs={{0,8},{1,9},{2,10},{3,11},{4,12},{5,13},{6,14},{7,15},{8,0},{9,1},... | collective-permute-start | bytes 786440 | tf_op jit(solution)/shard_map/ppermute | solution.py:473
  106.3 39.4 %collective-permute-start.10 = (bf16[128,1024]{1,0:T(8,128)(2,1)}, bf16[128,1024]{1,0:T(8,128)(2,1)S(1)}, u32[]{:S(2)}, u32[]{:S(2)}) collective-permute-start(bf16[128,1024]{1,0:T(8,128)(2,1)} %get-tuple-element.34), channel_id=1, source_target_pairs={{0,9},{1,10},{2,11},{3,8},{4,13},{5,14},{6,15},{7,12},{8,1},{9,2},... | collective-permute-start | bytes 786440 | tf_op jit(solution)/shard_map/ppermute | solution.py:473
  118.7 27.0 %collective-permute-start.11 = (bf16[128,1024]{1,0:T(8,128)(2,1)}, bf16[128,1024]{1,0:T(8,128)(2,1)S(1)}, u32[]{:S(2)}, u32[]{:S(2)}) collective-permute-start(bf16[128,1024]{1,0:T(8,128)(2,1)} %get-tuple-element.35), channel_id=1, source_target_pairs={{0,10},{1,11},{2,8},{3,9},{4,14},{5,15},{6,12},{7,13},{8,2},{9,3},... | collective-permute-start | bytes 786440 | tf_op jit(solution)/shard_map/ppermute | solution.py:473
  128.3 62.5 %collective-permute-start.12 = (bf16[128,1024]{1,0:T(8,128)(2,1)}, bf16[128,1024]{1,0:T(8,128)(2,1)S(1)}, u32[]{:S(2)}, u32[]{:S(2)}) collective-permute-start(bf16[128,1024]{1,0:T(8,128)(2,1)} %get-tuple-element.36), channel_id=1, source_target_pairs={{0,11},{1,8},{2,9},{3,10},{4,15},{5,12},{6,13},{7,14},{8,3},{9,0},... | collective-permute-start | bytes 786440 | tf_op jit(solution)/shard_map/ppermute | solution.py:473
  145.7 45.0 %collective-permute-start.13 = (bf16[128,1024]{1,0:T(8,128)(2,1)}, bf16[128,1024]{1,0:T(8,128)(2,1)S(1)}, u32[]{:S(2)}, u32[]{:S(2)}) collective-permute-start(bf16[128,1024]{1,0:T(8,128)(2,1)} %get-tuple-element.37), channel_id=1, source_target_pairs={{0,12},{1,13},{2,14},{3,15},{4,0},{5,1},{6,2},{7,3},{8,4},{9,5},{1... | collective-permute-start | bytes 786440 | tf_op jit(solution)/shard_map/ppermute | solution.py:473
  145.7 45.1 %collective-permute-start.14 = (bf16[128,1024]{1,0:T(8,128)(2,1)}, bf16[128,1024]{1,0:T(8,128)(2,1)S(1)}, u32[]{:S(2)}, u32[]{:S(2)}) collective-permute-start(bf16[128,1024]{1,0:T(8,128)(2,1)} %get-tuple-element.38), channel_id=1, source_target_pairs={{0,13},{1,14},{2,15},{3,12},{4,1},{5,2},{6,3},{7,0},{8,5},{9,6},{1... | collective-permute-start | bytes 786440 | tf_op jit(solution)/shard_map/ppermute | solution.py:473
  145.8 45.0 %collective-permute-start.15 = (bf16[128,1024]{1,0:T(8,128)(2,1)}, bf16[128,1024]{1,0:T(8,128)(2,1)S(1)}, u32[]{:S(2)}, u32[]{:S(2)}) collective-permute-start(bf16[128,1024]{1,0:T(8,128)(2,1)} %get-tuple-element.39), channel_id=1, source_target_pairs={{0,14},{1,15},{2,12},{3,13},{4,2},{5,3},{6,0},{7,1},{8,6},{9,7},{1... | collective-permute-start | bytes 786440 | tf_op jit(solution)/shard_map/ppermute | solution.py:473
  148.7 42.1 %collective-permute-start.16 = (bf16[128,1024]{1,0:T(8,128)(2,1)}, bf16[128,1024]{1,0:T(8,128)(2,1)S(1)}, u32[]{:S(2)}, u32[]{:S(2)}) collective-permute-start(bf16[128,1024]{1,0:T(8,128)(2,1)} %get-tuple-element.40), channel_id=1, source_target_pairs={{0,15},{1,12},{2,13},{3,14},{4,3},{5,0},{6,1},{7,2},{8,7},{9,4},{1... | collective-permute-start | bytes 786440 | tf_op jit(solution)/shard_map/ppermute | solution.py:473
